TPU v7x, 256 devices: a 4x2x16 block of a 4x16x16 slice. The times are simulated.
256 devices in a mesh: ga: 2 (over y), ea: 128 (over z, x, core).
Axes of the slice: x: 4, y: 2, z: 16, core: 2. Of those that a mesh axis runs over, the one named last changes fastest.
The devices are a block of a 4x16x16 slice.
Arguments:
- tokens: bfloat16 [32768, 2048], P(('ga', 'ea')), parts along dimension 0, may hold values from -6 to 6
- expert_choice_index: int32 [32768, 4], P(('ga', 'ea')), parts along dimension 0, may hold values from 0 to 63, all different within a row; in each aligned block of 128 rows (0 to 127, 128 to 255, ...) at most 9 rows name the same one
- router_gate_weight: float32 [32768, 4], P(('ga', 'ea')), parts along dimension 0, may hold values from 0.05 to 0.6
- cotangent: bfloat16 [32768, 2048], P(('ga', 'ea')), parts along dimension 0, may hold values from -6 to 6
- gate_up_matrix: bfloat16 [128, 2048, 1408], P('ea'), may hold values from -0.125 to 0.125
- down_weight: bfloat16 [128, 704, 2048], P('ea'), may hold values from -0.15625 to 0.15625
- adapter_input_projection: bfloat16 [2048, 16], replicated, may hold values from -0.125 to 0.125
- adapter_output_projection: bfloat16 [128, 16, 1408], P('ea'), may hold values from -0.59765625 to 0.59765625
Outputs:
- layer_output: bfloat16 [32768, 2048], P(('ga', 'ea')), parts along dimension 0
- adapter_input_gradient: float32 [4096, 16], P('ga'), parts along dimension 0
- lora_b_grad: float32 [256, 16, 1408], P(('ga', 'ea')), parts along dimension 0
There are 2 independent parts, one for each index of `ga`. A program takes and returns all parts, laid end to end along the dimension named above; an argument that names none is the same for every part. Nothing has to cross between parts.
Inputs may be any that keep to these rules, and one draw needn't show every extreme that they name: `expert_choice_index`: each row names 4 different experts. Within the rows of one device (aligned blocks of 128 rows) no expert is named by more than 9 rows, and in every draw some expert is named by exactly 9 rows of some block.
All inputs are finite; a program needn't handle non-finite values.
Results may differ from a plain program's by a relative error of at most 0.0072.
Values may be sent and summed in bfloat16 or wider, within the bound.
No kernel may reach another device: no remote copies, remote signals or barrier semaphores. Data moves between devices by JAX's collectives and lax.ppermute only.
A program may use at most 128 MiB of HBM per device.

v0:
```python
import jax
import jax.numpy as jnp
from jax import lax
from jax.sharding import Mesh
from jax.sharding import PartitionSpec as P

EXPERT_SPLIT = 2
EA = ("ea_0", "ea_1", "ea_2")
GA_EA = ("ga", "ea_0", "ea_1", "ea_2")
adapter_scale = 2.0


def from_partner(value, axis, distance):
    mask = 2**distance
    pairs = [(source, source ^ mask) for source in range(lax.axis_size(axis))]
    return lax.ppermute(value, axis, pairs)


def one_axis_at_a_time(array, axes):
    for axis in axes:
        array = lax.psum(array, axis)
    return array


def slot_ranks(id_block, experts):
    flat_ids = id_block.reshape(-1)
    onehot = (flat_ids[:, None] == jnp.arange(experts, dtype=jnp.int32)[None, :]).astype(jnp.int32)
    before = jnp.cumsum(onehot, axis=0) - onehot
    return jnp.sum(before * onehot, axis=1).reshape(id_block.shape)


def block_halfway(
    input_rows, output_gradient_rows, gate_up_weight, down_w, adapter_a, adapter_output_weight
):
    adapter_input_rows = jnp.dot(input_rows, adapter_a, preferred_element_type=jnp.float32).astype(
        jnp.bfloat16
    )
    joined_columns = jnp.dot(
        input_rows, gate_up_weight, preferred_element_type=jnp.float32
    ) + adapter_scale * jnp.dot(
        adapter_input_rows, adapter_output_weight, preferred_element_type=jnp.float32
    )
    block_width = down_w.shape[0]
    gate_part = joined_columns[:, :block_width]
    up_part = joined_columns[:, block_width:]
    sigmoid_gate = jax.nn.sigmoid(gate_part)
    active = gate_part * sigmoid_gate
    hidden = (active * up_part).astype(jnp.bfloat16)
    partial_value = jnp.dot(hidden, down_w, preferred_element_type=jnp.float32).astype(jnp.bfloat16)
    down_grad = lax.dot_general(
        output_gradient_rows, down_w, (((1,), (1,)), ((), ())), preferred_element_type=jnp.float32
    )
    gate_grad = down_grad * up_part * sigmoid_gate * (1.0 + gate_part * (1.0 - sigmoid_gate))
    up_grad = down_grad * active
    joined_gradient = jnp.concatenate([gate_grad, up_grad], axis=1).astype(jnp.bfloat16)
    output_gradient_part = adapter_scale * lax.dot_general(
        adapter_input_rows,
        joined_gradient,
        (((0,), (0,)), ((), ())),
        preferred_element_type=jnp.float32,
    )
    adapter_gradient = (
        adapter_scale
        * lax.dot_general(
            joined_gradient,
            adapter_output_weight,
            (((1,), (1,)), ((), ())),
            preferred_element_type=jnp.float32,
        )
    ).astype(jnp.bfloat16)
    grad_a = lax.dot_general(
        input_rows, adapter_gradient, (((0,), (0,)), ((), ())), preferred_element_type=jnp.float32
    )
    return (partial_value, grad_a, output_gradient_part)


def local(
    tokens,
    expert_choice_index,
    router_gate_weight,
    cotangent,
    gate_up_matrix,
    down_weight,
    adapter_input_projection,
    adapter_output_projection,
):
    devices = lax.axis_size(EA)
    experts = devices // EXPERT_SPLIT
    tok_rows, model_width = tokens.shape
    top_count = expert_choice_index.shape[1]
    capacity = 9 * tok_rows * top_count // (8 * experts)
    half_width = model_width // 2
    parity = lax.axis_index(EA) % 2
    slot_rank = slot_ranks(expert_choice_index, experts)
    slot_rows = (expert_choice_index * capacity + slot_rank).reshape(-1)
    scaled_dy = (router_gate_weight[:, :, None] * cotangent[:, None, :].astype(jnp.float32)).astype(
        jnp.bfloat16
    )
    repeated = jnp.broadcast_to(tokens[:, None, :], (tok_rows, top_count, model_width))
    both_rows = jnp.stack([repeated, scaled_dy], axis=2).reshape(
        tok_rows * top_count, 2, model_width
    )
    blank_rows = jnp.zeros((experts * capacity, 2, model_width), jnp.bfloat16)
    send_rows = blank_rows.at[slot_rows].set(both_rows, unique_indices=True)
    rows_total = devices * capacity
    halves = (
        send_rows.reshape(experts, capacity, 2, 2, half_width)
        .transpose(0, 3, 1, 2, 4)
        .reshape(devices, capacity, 2, half_width)
    )
    own_piece = lax.all_to_all(halves, EA, split_axis=0, concat_axis=0, tiled=True)
    other_piece = from_partner(own_piece, EA, 0)
    lower_block_part = jnp.where(parity == 0, own_piece, other_piece)
    upper_block_part = jnp.where(parity == 0, other_piece, own_piece)
    arrived = jnp.concatenate([lower_block_part, upper_block_part], axis=3)
    input_rows = arrived[:, :, 0].reshape(rows_total, model_width)
    output_gradient_rows = arrived[:, :, 1].reshape(rows_total, model_width)
    partial_value, input_gradient_local, output_gradient_part = block_halfway(
        input_rows,
        output_gradient_rows,
        gate_up_matrix[0],
        down_weight[0],
        adapter_input_projection,
        adapter_output_projection[0],
    )
    adapter_input_gradient = one_axis_at_a_time(input_gradient_local, EA)
    partial_value = partial_value.reshape(devices, capacity, model_width)
    kept_part = jnp.where(
        parity == 0, partial_value[:, :, :half_width], partial_value[:, :, half_width:]
    )
    given_part = jnp.where(
        parity == 0, partial_value[:, :, half_width:], partial_value[:, :, :half_width]
    )
    taken_part = from_partner(given_part, EA, 0)
    summed = (kept_part.astype(jnp.float32) + taken_part.astype(jnp.float32)).astype(jnp.bfloat16)
    returned = lax.all_to_all(summed, EA, split_axis=0, concat_axis=0, tiled=True)
    expert_out = (
        returned.reshape(experts, 2, capacity, half_width)
        .transpose(0, 2, 1, 3)
        .reshape(experts * capacity, model_width)
    )
    picked = expert_out[slot_rows].reshape(tok_rows, top_count, model_width).astype(jnp.float32)
    layer_output = jnp.sum(router_gate_weight[:, :, None] * picked, axis=1).astype(jnp.bfloat16)
    return (layer_output, adapter_input_gradient, output_gradient_part[None])


def solution(mesh):
    split = Mesh(mesh.devices.reshape(mesh.shape["ga"], 16, 4, 2), ("ga", "ea_0", "ea_1", "ea_2"))
    in_specs = (
        P(GA_EA, None),
        P(GA_EA, None),
        P(GA_EA, None),
        P(GA_EA, None),
        P(EA, None, None),
        P(EA, None, None),
        P(),
        P(EA, None, None),
    )
    out_specs = (P(GA_EA, None), P("ga", None), P(GA_EA, None, None))
    return jax.shard_map(local, mesh=split, in_specs=in_specs, out_specs=out_specs, check_vma=False)
```

profile of v0, /device:TPU:33, one launch (start us, length us, event | category | flops | bytes accessed | tf_op | source)
XLA Modules:
  0.0 807.9 jit_solution(12720040110281030694)
XLA Ops:
  16.2 5.3 mul.96
  33.0 8.5 %copy.75 = bf16[512,2,2048]{2,1,0:T(2,128)(2,1)} copy(bf16[512,2,2048]{2,0,1:T(8,128)(2,1)} %pad_maximum_fusion.1) | data formatting | bytes 8388608 | tf_op jit(solution)/shard_map/stack | solution.py:100
  46.1 64.3 %scatter_fusion = bf16[576,2,2048]{2,1,0:T(2,128)(2,1)} fusion(bf16[576,2,2048]{2,1,0:T(2,128)(2,1)} %broadcast_in_dim.4, s32[512]{0:T(512)S(1)} %bitcast.57, bf16[512,2,2048]{2,1,0:T(2,128)(2,1)} %copy.75), kind=kCustom, calls=%fused_computation.1 | custom fusion | bytes 12584960 | tf_op jit(solution)/shard_map/scatter | solution.py:104
  110.4 13.7 %reshape.146 = bf16[64,9,2,2,1024]{4,3,2,1,0:T(2,128)(2,1)} reshape(bf16[576,2,2048]{2,1,0:T(2,128)(2,1)} %scatter_fusion) | data formatting | bytes 9437184 | tf_op jit(solution)/shard_map/reshape | solution.py:107
  124.0 8.3 %copy.77 = bf16[64,2,9,2,1024]{4,3,2,1,0:T(2,128)(2,1)} copy(bf16[64,2,9,2,1024]{4,1,3,2,0:T(2,128)(2,1)} %bitcast.54) | data formatting | bytes 9437184 | tf_op jit(solution)/shard_map/transpose | solution.py:108
  132.3 242.0 %all_to_all.10 = bf16[128,9,2,1024]{3,2,1,0:T(2,128)(2,1)} all-to-all(bf16[128,9,2,1024]{3,2,1,0:T(2,128)(2,1)} %bitcast.55), channel_id=1, replica_groups=mesh['ga'=2,'ea_0'=16,'ea_1'=4,'ea_2'=2] {'ea_0','ea_1','ea_2'}, dimensions={0} | all-to-all | bytes 9437184 | tf_op jit(solution)/shard_map/all_to_all | solution.py:111
  374.6 7.9 collective-permute-done
  382.6 10.9 %broadcast_select_fusion.1 = (bf16[128,9,2,1024]{3,2,1,0:T(2,128)(2,1)}, bf16[128,9,2,1024]{3,2,1,0:T(2,128)(2,1)}) fusion(bf16[128,9,2,1024]{3,2,1,0:T(2,128)(2,1)} %all_to_all.10, bf16[128,9,2,1024]{3,2,1,0:T(2,128)(2,1)} %collective-permute-done, pred[]{:T(512)S(6)} %eq.33), kind=kLoop, calls=%fused_computation.8 | loop fusion | flops 4718592 | bytes 18874368 | tf_op jit(solution)/shard_map/jit(_where)/select_n | solution.py:113
  393.5 65.1 %fusion.1 = (bf16[128,9,2048]{2,1,0:T(8,128)(2,1)}, bf16[128,9,2048]{2,1,0:T(8,128)(2,1)}) fusion(bf16[128,9,2,1024]{3,2,1,0:T(2,128)(2,1)} %get-tuple-element.8, bf16[128,9,2,1024]{3,2,1,0:T(2,128)(2,1)} %get-tuple-element.7), kind=kLoop, calls=%fused_computation.6 | loop fusion | flops 18874368 | bytes 18874368 | tf_op jit(solution)/shard_map/slice | solution.py:117
  458.5 8.5 %reshape_squeeze.6 = bf16[1152,2048]{1,0:T(8,128)(2,1)} reshape(bf16[128,9,2048]{2,1,0:T(8,128)(2,1)} %get-tuple-element.4) | data formatting | bytes 9437184 | tf_op jit(solution)/shard_map/reshape;squeeze | solution.py:116
  467.1 11.9 %fusion.2 = f32[1152,1408]{1,0:T(8,128)S(1)} fusion(bf16[1152,2048]{1,0:T(8,128)(2,1)} %reshape_squeeze.6, bf16[1,2048,1408]{2,1,0:T(8,128)(2,1)} %param.12), kind=kOutput, calls=%fused_computation.10 | convolution fusion | flops 6643777536 | bytes 16973824 | tf_op jit(solution)/shard_map/dot_general | solution.py:38
  484.1 5.6 convolution_convert_fusion
  489.8 8.1 %reshape.126 = bf16[128,9,2048]{2,1,0:T(8,128)(2,1)} reshape(bf16[1152,2048]{1,0:T(8,128)(2,1)} %convolution_convert_fusion) | data formatting | bytes 9437184 | tf_op jit(solution)/shard_map/reshape | solution.py:127
  501.8 5.0 broadcast_select_fusion.2
  519.0 9.9 %all-to-all-start.1 = ((bf16[128,9,1024]{2,1,0:T(8,128)(2,1)}), bf16[128,9,1024]{2,1,0:T(8,128)(2,1)}, u32[]{:S(2)}, u32[]{:S(2)}) async-start(bf16[128,9,1024]{2,1,0:T(8,128)(2,1)} %copy.80), calls=%async_computation.1 | async-start | bytes 8388608 | tf_op jit(solution)/shard_map/all_to_all | solution.py:136
  529.2 8.5 %reshape_squeeze.7 = bf16[1152,2048]{1,0:T(8,128)(2,1)} reshape(bf16[128,9,2048]{2,1,0:T(8,128)(2,1)} %get-tuple-element.3) | data formatting | bytes 9437184 | tf_op jit(solution)/shard_map/reshape;squeeze | solution.py:117
  537.7 11.1 %multiply_convert_fusion.2 = (bf16[1152,704]{1,0:T(8,128)(2,1)}, bf16[1152,704]{1,0:T(8,128)(2,1)}) fusion(f32[1152,1408]{1,0:T(8,128)} %copy-done.3, bf16[1152,2048]{1,0:T(8,128)(2,1)} %reshape_squeeze.7, bf16[1,704,2048]{2,1,0:T(8,128)(2,1)S(1)} %copy-done), kind=kOutput, calls=%fused_computation.17 | convolution fusion | flops 3332431872 | bytes 17334272 | tf_op jit(solution)/shard_map/dot_general | solution.py:50
  548.8 5.9 fusion.10
  554.8 145.5 %all-reduce.4.cloned.1.call-done = f32[2048,16]{0,1:T(8,128)} async-done(((f32[2048,16]{0,1:T(8,128)}), f32[2048,16]{0,1:T(8,128)}) %all-reduce.4.cloned.1.call-update) | async-done | bytes 131088 | tf_op jit(solution)/shard_map/psum | solution.py:21
  704.4 53.2 %all-reduce.6.cloned.1.call-done = f32[2048,16]{0,1:T(8,128)} async-done(((f32[2048,16]{0,1:T(8,128)}), f32[2048,16]{0,1:T(8,128)}) %all-reduce.6.cloned.1.call-update) | async-done | bytes 131088 | tf_op jit(solution)/shard_map/psum | solution.py:21
  757.6 4.9 copy.81
  764.6 7.2 gather_fusion
  776.5 6.2 multiply_reduce_fusion
  782.8 16.8 %all-reduce.8.cloned.1.call-done = f32[2048,16]{0,1:T(8,128)} async-done(((f32[2048,16]{0,1:T(8,128)}), f32[2048,16]{0,1:T(8,128)}) %all-reduce.8.cloned.1.call-update) | async-done | bytes 131088 | tf_op jit(solution)/shard_map/psum | solution.py:21
  (57 shorter events, 59.5 us)
Async XLA Ops:
  7.2 477.0 %copy-start = (bf16[1,704,2048]{2,1,0:T(8,128)(2,1)S(1)}, bf16[1,704,2048]{2,1,0:T(8,128)(2,1)}, u32[]{:S(2)}) copy-start(bf16[1,704,2048]{2,1,0:T(8,128)(2,1)} %param.13) | copy-start | bytes 8650756
  16.2 5.3 copy-start.4
  27.9 2.9 copy-start.2
  374.3 8.3 %collective-permute-start = (bf16[128,9,2,1024]{3,2,1,0:T(2,128)(2,1)}, bf16[128,9,2,1024]{3,2,1,0:T(2,128)(2,1)}, u32[]{:S(2)}, u32[]{:S(2)}) collective-permute-start(bf16[128,9,2,1024]{3,2,1,0:T(2,128)(2,1)} %all_to_all.10), channel_id=1, source_target_pairs={{0,1},{1,0},{2,3},{3,2},{4,5},{5,4},{6,7},{7,6},{8,9},{9,8},{10,11... | collective-permute-start | bytes 14155784 | tf_op jit(solution)/shard_map/ppermute | solution.py:16
  467.1 11.9 %copy-start.1 = (bf16[1152,2048]{1,0:T(8,128)(2,1)S(1)}, bf16[1152,2048]{1,0:T(8,128)(2,1)}, u32[]{:S(2)}) copy-start(bf16[1152,2048]{1,0:T(8,128)(2,1)} %reshape_squeeze.6) | copy-start | bytes 14155780
  467.1 11.9 %copy-start.6 = (bf16[2048,16]{0,1:T(8,128)(2,1)S(1)}, bf16[2048,16]{0,1:T(8,128)(2,1)}, u32[]{:S(2)}) copy-start(bf16[2048,16]{0,1:T(8,128)(2,1)} %param.14) | copy-start | bytes 196612
  479.0 1.3 copy-start.5
  481.4 2.8 copy-start.3
  506.9 4.9 collective-permute-start.1
  519.0 238.6 %all-to-all-start.1 = ((bf16[128,9,1024]{2,1,0:T(8,128)(2,1)}), bf16[128,9,1024]{2,1,0:T(8,128)(2,1)}, u32[]{:S(2)}, u32[]{:S(2)}) async-start(bf16[128,9,1024]{2,1,0:T(8,128)(2,1)} %copy.80), calls=%async_computation.1 | async-start | bytes 8388608 | tf_op jit(solution)/shard_map/all_to_all | solution.py:136
  528.9 171.5 %all-reduce.4.cloned.1.call-start = ((), (), s32[]{:S(2)}) async-start(), calls=%async_computation.2 | async-start | bytes 262144 | tf_op jit(solution)/shard_map/psum | solution.py:21
  554.8 202.8 %all-reduce.6.cloned.1.call-start = ((), (), s32[]{:S(2)}) async-start(), calls=%async_computation.3 | async-start | bytes 262144 | tf_op jit(solution)/shard_map/psum | solution.py:21
  700.4 99.2 %all-reduce.8.cloned.1.call-start = ((), (), s32[]{:S(2)}) async-start(), calls=%async_computation.4 | async-start | bytes 262144 | tf_op jit(solution)/shard_map/psum | solution.py:21
Sparse Core Ops, SparseCore 0:
  554.9 145.3 all-reduce.3
  702.7 54.8 all-reduce.5
  760.1 39.4 all-reduce.7
where the time goes:
time: 819 us; the launch traced here: 808 us
  blocking collectives  242 us (30%)
  waiting for transfers between devices  228 us (28%)
  local copies, waits for them, and re-layouts  174 us (21%)
  other arithmetic  97.9 us (12%)
  matrix products  40.3 us (5%)
  between operations  14.1 us (2%)
  starting transfers between devices  11.7 us (1%)
    all_to_all x1, blocking collectives, local(): lax.all_to_all(halves, EA, split_axis=0, concat_axis=0, tiled=True)  242 us
    psum x3, waiting for transfers between devices, one_axis_at_a_time(): array = lax.psum(array, axis)  215 us
    slice x1, other arithmetic, local(): output_gradient_rows = arrived[:, :, 1].reshape(rows_total, model_width)  65.1 us
    scatter x1, local copies, waits for them, and re-layouts, local(): send_rows = blank_rows.at[slot_rows].set(both_rows, unique_indices=True)  64.3 us
  transfers between devices with their start and end apart: 6, of which 5 were waited for; matrix products, arithmetic and copies ran while one was open for 7% of the time, Pallas kernels for 0%

commit v1 on v0

--- a/solution.py
+++ b/solution.py
@@ -18,7 +18,7 @@
 
 def one_axis_at_a_time(array, axes):
     for axis in axes:
-        array = lax.psum(array, axis)
+        array = jnp.sum(lax.all_gather(array, axis), axis=0)
     return array
 
 

time: 819 us -> 781 us (0.954)
  the two profiles are of different devices: /device:TPU:33 before, /device:TPU:40 now
where the time goes in v1:
time: 781 us; the launch traced here: 770 us
  blocking collectives  275 us (35%)
  local copies, waits for them, and re-layouts  177 us (23%)
  waiting for transfers between devices  150 us (19%)
  other arithmetic  100 us (13%)
  matrix products  40.4 us (5%)
  between operations  14.5 us (2%)
  starting transfers between devices  13.3 us (2%)
    all_to_all x1, blocking collectives, local(): lax.all_to_all(halves, EA, split_axis=0, concat_axis=0, tiled=True)  241 us
    all_gather x1, waiting for transfers between devices, one_axis_at_a_time(): array = jnp.sum(lax.all_gather(array, axis), axis=0)  124 us
    slice x1, other arithmetic, local(): output_gradient_rows = arrived[:, :, 1].reshape(rows_total, model_width)  65.1 us
    scatter x1, local copies, waits for them, and re-layouts, local(): send_rows = blank_rows.at[slot_rows].set(both_rows, unique_indices=True)  64.2 us
    all_gather x2, blocking collectives, one_axis_at_a_time(): array = jnp.sum(lax.all_gather(array, axis), axis=0)  34.1 us
  transfers between devices with their start and end apart: 4, of which 4 were waited for; matrix products, arithmetic and copies ran while one was open for 5% of the time, Pallas kernels for 0%

profile of v1, /device:TPU:40, one launch (start us, length us, event | category | flops | bytes accessed | tf_op | source)
XLA Modules:
  0.0 770.3 jit_solution(14020321876487825296)
XLA Ops:
  16.2 5.3 mul.96
  33.0 8.5 %copy.90 = bf16[512,2,2048]{2,1,0:T(2,128)(2,1)} copy(bf16[512,2,2048]{2,0,1:T(8,128)(2,1)} %pad_maximum_fusion.1) | data formatting | bytes 8388608 | tf_op jit(solution)/shard_map/stack | solution.py:100
  46.1 64.2 %scatter_fusion = bf16[576,2,2048]{2,1,0:T(2,128)(2,1)} fusion(bf16[576,2,2048]{2,1,0:T(2,128)(2,1)} %broadcast_in_dim.4, s32[512]{0:T(512)S(1)} %bitcast.67, bf16[512,2,2048]{2,1,0:T(2,128)(2,1)} %copy.90), kind=kCustom, calls=%fused_computation.1 | custom fusion | bytes 12584960 | tf_op jit(solution)/shard_map/scatter | solution.py:104
  110.3 13.9 %reshape.149 = bf16[64,9,2,2,1024]{4,3,2,1,0:T(2,128)(2,1)} reshape(bf16[576,2,2048]{2,1,0:T(2,128)(2,1)} %scatter_fusion) | data formatting | bytes 9437184 | tf_op jit(solution)/shard_map/reshape | solution.py:107
  124.2 8.3 %copy.92 = bf16[64,2,9,2,1024]{4,3,2,1,0:T(2,128)(2,1)} copy(bf16[64,2,9,2,1024]{4,1,3,2,0:T(2,128)(2,1)} %bitcast.63) | data formatting | bytes 9437184 | tf_op jit(solution)/shard_map/transpose | solution.py:108
  132.5 240.9 %all_to_all.10 = bf16[128,9,2,1024]{3,2,1,0:T(2,128)(2,1)} all-to-all(bf16[128,9,2,1024]{3,2,1,0:T(2,128)(2,1)} %bitcast.64), channel_id=1, replica_groups=mesh['ga'=2,'ea_0'=16,'ea_1'=4,'ea_2'=2] {'ea_0','ea_1','ea_2'}, dimensions={0} | all-to-all | bytes 9437184 | tf_op jit(solution)/shard_map/all_to_all | solution.py:111
  373.6 8.0 %collective-permute-done = bf16[128,9,2,1024]{3,2,1,0:T(2,128)(2,1)} collective-permute-done((bf16[128,9,2,1024]{3,2,1,0:T(2,128)(2,1)}, bf16[128,9,2,1024]{3,2,1,0:T(2,128)(2,1)}, u32[]{:S(2)}, u32[]{:S(2)}) %collective-permute-start) | collective-permute-done | bytes 4718624 | tf_op jit(solution)/shard_map/ppermute | solution.py:16
  381.7 10.6 %broadcast_select_fusion.1 = (bf16[128,9,2,1024]{3,2,1,0:T(2,128)(2,1)}, bf16[128,9,2,1024]{3,2,1,0:T(2,128)(2,1)}) fusion(bf16[128,9,2,1024]{3,2,1,0:T(2,128)(2,1)} %all_to_all.10, bf16[128,9,2,1024]{3,2,1,0:T(2,128)(2,1)} %collective-permute-done, pred[]{:T(512)S(6)} %eq.33), kind=kLoop, calls=%fused_computation.8 | loop fusion | flops 4718592 | bytes 18874368 | tf_op jit(solution)/shard_map/jit(_where)/select_n | solution.py:113
  392.3 65.1 %fusion.1 = (bf16[128,9,2048]{2,1,0:T(8,128)(2,1)}, bf16[128,9,2048]{2,1,0:T(8,128)(2,1)}) fusion(bf16[128,9,2,1024]{3,2,1,0:T(2,128)(2,1)} %get-tuple-element.8, bf16[128,9,2,1024]{3,2,1,0:T(2,128)(2,1)} %get-tuple-element.7), kind=kLoop, calls=%fused_computation.6 | loop fusion | flops 18874368 | bytes 18874368 | tf_op jit(solution)/shard_map/slice | solution.py:117
  457.4 8.5 %reshape_squeeze.6 = bf16[1152,2048]{1,0:T(8,128)(2,1)} reshape(bf16[128,9,2048]{2,1,0:T(8,128)(2,1)} %get-tuple-element.4) | data formatting | bytes 9437184 | tf_op jit(solution)/shard_map/reshape;squeeze | solution.py:116
  465.9 11.9 %fusion.2 = f32[1152,1408]{1,0:T(8,128)S(1)} fusion(bf16[1152,2048]{1,0:T(8,128)(2,1)} %reshape_squeeze.6, bf16[1,2048,1408]{2,1,0:T(8,128)(2,1)} %param.12), kind=kOutput, calls=%fused_computation.10 | convolution fusion | flops 6643777536 | bytes 16973824 | tf_op jit(solution)/shard_map/dot_general | solution.py:38
  483.0 5.6 convolution_convert_fusion
  488.6 8.0 %reshape.126 = bf16[128,9,2048]{2,1,0:T(8,128)(2,1)} reshape(bf16[1152,2048]{1,0:T(8,128)(2,1)} %convolution_convert_fusion) | data formatting | bytes 9437184 | tf_op jit(solution)/shard_map/reshape | solution.py:127
  500.6 5.0 broadcast_select_fusion.2
  517.9 12.2 %all-to-all-start.1 = ((bf16[128,9,1024]{2,1,0:T(8,128)(2,1)}), bf16[128,9,1024]{2,1,0:T(8,128)(2,1)}, u32[]{:S(2)}, u32[]{:S(2)}) async-start(bf16[128,9,1024]{2,1,0:T(8,128)(2,1)} %copy.95), calls=%async_computation.1 | async-start | bytes 8388608 | tf_op jit(solution)/shard_map/all_to_all | solution.py:136
  530.3 8.5 %reshape_squeeze.7 = bf16[1152,2048]{1,0:T(8,128)(2,1)} reshape(bf16[128,9,2048]{2,1,0:T(8,128)(2,1)} %get-tuple-element.3) | data formatting | bytes 9437184 | tf_op jit(solution)/shard_map/reshape;squeeze | solution.py:117
  538.8 11.1 %multiply_convert_fusion.2 = (bf16[1152,704]{1,0:T(8,128)(2,1)}, bf16[1152,704]{1,0:T(8,128)(2,1)}) fusion(f32[1152,1408]{1,0:T(8,128)} %copy-done.3, bf16[1152,2048]{1,0:T(8,128)(2,1)} %reshape_squeeze.7, bf16[1,704,2048]{2,1,0:T(8,128)(2,1)S(1)} %copy-done), kind=kOutput, calls=%fused_computation.17 | convolution fusion | flops 3332431872 | bytes 17334272 | tf_op jit(solution)/shard_map/dot_general | solution.py:50
  549.9 5.9 fusion.10
  559.4 124.2 %all-gather.5.cloned.1.call-done = f32[32768,16]{0,1:T(8,128)} async-done(((f32[2048,16]{0,1:T(8,128)}), f32[32768,16]{0,1:T(8,128)}) %all-gather.5.cloned.1.call-update) | async-done | bytes 2097168 | tf_op jit(solution)/shard_map/all_gather | solution.py:21
  686.8 31.9 %all-gather.1 = f32[8192,16]{0,1:T(8,128)S(1)} all-gather(f32[2048,16]{0,1:T(8,128)S(1)} %bitcast_reduce_fusion), channel_id=3, replica_groups=mesh['ga'=2,'ea_0'=16,'ea_1'=4,'ea_2'=2] {'ea_1'}, dimensions={0}, use_global_device_ids=true | all-gather | bytes 655360 | tf_op jit(solution)/shard_map/all_gather | solution.py:21
  724.6 13.3 %all-to-all-done.1 = bf16[128,9,1024]{2,1,0:T(8,128)(2,1)} async-done(((bf16[128,9,1024]{2,1,0:T(8,128)(2,1)}), bf16[128,9,1024]{2,1,0:T(8,128)(2,1)}, u32[]{:S(2)}, u32[]{:S(2)}) %all-to-all-start.1) | async-done | bytes 2359328 | tf_op jit(solution)/shard_map/all_to_all | solution.py:136
  738.0 4.9 copy.96
  744.9 7.3 gather_fusion
  757.0 6.2 multiply_reduce_fusion
  (58 shorter events, 66.4 us)
Async XLA Ops:
  7.2 475.8 %copy-start = (bf16[1,704,2048]{2,1,0:T(8,128)(2,1)S(1)}, bf16[1,704,2048]{2,1,0:T(8,128)(2,1)}, u32[]{:S(2)}) copy-start(bf16[1,704,2048]{2,1,0:T(8,128)(2,1)} %param.13) | copy-start | bytes 8650756
  16.2 5.3 copy-start.4
  27.9 2.9 copy-start.2
  373.4 8.3 %collective-permute-start = (bf16[128,9,2,1024]{3,2,1,0:T(2,128)(2,1)}, bf16[128,9,2,1024]{3,2,1,0:T(2,128)(2,1)}, u32[]{:S(2)}, u32[]{:S(2)}) collective-permute-start(bf16[128,9,2,1024]{3,2,1,0:T(2,128)(2,1)} %all_to_all.10), channel_id=1, source_target_pairs={{0,1},{1,0},{2,3},{3,2},{4,5},{5,4},{6,7},{7,6},{8,9},{9,8},{10,11... | collective-permute-start | bytes 14155784 | tf_op jit(solution)/shard_map/ppermute | solution.py:16
  465.9 11.9 %copy-start.1 = (bf16[1152,2048]{1,0:T(8,128)(2,1)S(1)}, bf16[1152,2048]{1,0:T(8,128)(2,1)}, u32[]{:S(2)}) copy-start(bf16[1152,2048]{1,0:T(8,128)(2,1)} %reshape_squeeze.6) | copy-start | bytes 14155780
  465.9 11.9 %copy-start.6 = (bf16[2048,16]{0,1:T(8,128)(2,1)S(1)}, bf16[2048,16]{0,1:T(8,128)(2,1)}, u32[]{:S(2)}) copy-start(bf16[2048,16]{0,1:T(8,128)(2,1)} %param.14) | copy-start | bytes 196612
  477.8 1.3 copy-start.5
  480.2 2.8 copy-start.3
  505.6 5.1 collective-permute-start.1
  517.9 220.0 %all-to-all-start.1 = ((bf16[128,9,1024]{2,1,0:T(8,128)(2,1)}), bf16[128,9,1024]{2,1,0:T(8,128)(2,1)}, u32[]{:S(2)}, u32[]{:S(2)}) async-start(bf16[128,9,1024]{2,1,0:T(8,128)(2,1)} %copy.95), calls=%async_computation.1 | async-start | bytes 8388608 | tf_op jit(solution)/shard_map/all_to_all | solution.py:136
  530.1 153.5 %all-gather.5.cloned.1.call-start = ((), (), s32[]{:S(2)}) async-start(), calls=%async_computation.2 | async-start | bytes 2228224 | tf_op jit(solution)/shard_map/all_gather | solution.py:21
Sparse Core Ops, SparseCore 0:
  556.0 127.5 all-gather.4
